TPU v7x, 32 devices: a whole 2x2x4 slice. The times are simulated.
32 devices in a mesh: tm: 8 (over z, y), tensor: 4 (over x, core).
Axes of the slice: x: 2, y: 2, z: 4, core: 2. Of those that a mesh axis runs over, the one named last changes fastest.
Arguments:
- frames_in: bfloat16 [8, 528, 1024], P('tm'), may hold values from -6 to 6
- frame_time: int32 [8], replicated, may hold values from 0 to 7, each once
- cond_count: int32 [8], replicated, may hold values from 0 to 2
- ln1_gain: float32 [2, 1024], replicated, may hold values from 0.5 to 1.5
- ln1_bias: float32 [2, 1024], replicated, may hold values from -1.75 to 1.75
- qkv_weight: bfloat16 [2, 3, 1024, 1024], P(None, None, None, 'tensor'), may hold values from -17 to 17
- qkv_bias: float32 [2, 3, 1024], P(None, None, 'tensor'), may hold values from -1.75 to 1.75
- out_weight: bfloat16 [2, 1024, 1024], P(None, 'tensor'), may hold values from -0.1875 to 0.1875
- out_bias: float32 [2, 1024], replicated, may hold values from -1.75 to 1.75
- ln2_gain: float32 [2, 1024], replicated, may hold values from 0.5 to 1.5
- ln2_bias: float32 [2, 1024], replicated, may hold values from -1.75 to 1.75
- fc1_weight: bfloat16 [2, 1024, 4096], P(None, None, 'tensor'), may hold values from -0.1875 to 0.1875
- fc1_bias: float32 [2, 4096], P(None, 'tensor'), may hold values from -3 to 3
- fc2_weight: bfloat16 [2, 4096, 1024], P(None, 'tensor'), may hold values from -0.09375 to 0.09375
- fc2_bias: float32 [2, 1024], replicated, may hold values from -1.75 to 1.75
Outputs:
- frames_out: bfloat16 [8, 528, 1024], P('tm', 'tensor')
Inputs may be any that keep to these rules, and one draw needn't show every extreme that they name: `frame_time`: every time index 0 to 7 appears once. `cond_count`: the valid action and state tokens of a frame are its first ones.
All inputs are finite; a program needn't handle non-finite values.
Results may differ from a plain program's by a relative error of at most 0.04.
Values may be sent and summed in bfloat16 or wider, within the bound.
A program may use at most 128 MiB of HBM per device.

v0:
```python
import jax
import jax.numpy as jnp
from jax import lax
from jax.sharding import PartitionSpec as P

D = 1024
HEADS = 16
PATCH_DEV = 64
COND = 2
LAYERS = 2


def layer_norm(inputs, gain_row, bias_row):
    center = jnp.mean(inputs, axis=-1, keepdims=True)
    spread = jnp.mean(jnp.square(inputs - center), axis=-1, keepdims=True)
    return (inputs - center) * lax.rsqrt(spread + 1e-06) * gain_row + bias_row


def piece_tables(frame_time, cond_count, piece_count, frame_split, piece_rows):
    cond_dev = COND // frame_split
    piece_ids = jnp.arange(piece_count, dtype=jnp.int32)
    frame_ids = jnp.arange(frame_time.shape[0], dtype=jnp.int32)
    matches = (piece_ids // frame_split)[:, None] == frame_ids[None, :]
    piece_time = jnp.sum(jnp.where(matches, frame_time[None, :], 0), axis=1)
    piece_cond = jnp.sum(jnp.where(matches, cond_count[None, :], 0), axis=1)
    slot_index = jnp.arange(piece_rows, dtype=jnp.int32)
    cond_slot = (piece_ids % frame_split)[:, None] * cond_dev + slot_index[None, :] - PATCH_DEV
    valid = (slot_index[None, :] < PATCH_DEV) | (cond_slot < piece_cond[:, None])
    return (piece_time, valid)


def shards_gather(
    frames_in,
    frame_time,
    cond_count,
    ln1_gain,
    ln1_bias,
    qkv_weight,
    qkv_bias,
    out_weight,
    out_bias,
    ln2_gain,
    ln2_bias,
    fc1_weight,
    fc1_bias,
    fc2_weight,
    fc2_bias,
):
    frame_count = frame_time.shape[0]
    piece_count = lax.axis_size("tm")
    frame_split = piece_count // frame_count
    cond_dev = COND // frame_split
    piece_rows = PATCH_DEV + cond_dev
    row_count = frames_in.shape[1]
    seq_count = row_count // piece_rows
    head_dim = D // HEADS
    head_local = qkv_weight.shape[3] // head_dim
    scale = head_dim ** (-0.5)
    tensor_size = lax.axis_size("tensor")
    tensor_pos = lax.axis_index("tensor")
    my_piece = lax.axis_index("tm")
    share_rows = row_count // tensor_size
    piece_time, valid = piece_tables(frame_time, cond_count, piece_count, frame_split, piece_rows)
    piece_ids = jnp.arange(piece_count, dtype=jnp.int32)
    my_time = jnp.sum(jnp.where(piece_ids == my_piece, piece_time, 0))
    full_in = frames_in[0]
    new_share = None
    for layer_idx in range(LAYERS):
        normed = layer_norm(
            full_in.astype(jnp.float32), ln1_gain[layer_idx], ln1_bias[layer_idx]
        ).astype(jnp.bfloat16)
        projected = jnp.einsum(
            "rd,jde->jre", normed, qkv_weight[layer_idx], preferred_element_type=jnp.float32
        )
        projected = (projected + qkv_bias[layer_idx][:, None, :]).astype(jnp.bfloat16)
        queries = projected[0].reshape(seq_count, piece_rows, head_local, head_dim)
        keys_mine = projected[1].reshape(1, seq_count, piece_rows, head_local * head_dim)
        values_mine = projected[2].reshape(1, seq_count, piece_rows, head_local * head_dim)
        start_top = jnp.full((seq_count, head_local, piece_rows), -1e30, jnp.float32)
        key_block = lax.all_gather(keys_mine, "tm", axis=0, tiled=True)
        value_block = lax.all_gather(values_mine, "tm", axis=0, tiled=True)
        block_count = key_block.shape[0]
        block_ids = jnp.arange(block_count, dtype=jnp.int32)
        matches = block_ids[:, None] == piece_ids[None, :]
        key_time = jnp.sum(jnp.where(matches, piece_time[None, :], 0), axis=1)
        key_valid = jnp.any(matches[:, :, None] & valid[None, :, :], axis=1)
        allowed = (key_time <= my_time)[:, None] & key_valid
        top_run = start_top
        keys_split = key_block.reshape(block_count, seq_count, piece_rows, head_local, head_dim)
        values_split = value_block.reshape(block_count, seq_count, piece_rows, head_local, head_dim)
        scores = (
            jnp.einsum("sqhd,gskhd->shqgk", queries, keys_split, preferred_element_type=jnp.float32)
            * scale
        )
        scores = jnp.where(allowed, scores, -1e30)
        new_top = jnp.maximum(top_run, jnp.max(scores, axis=(3, 4)))
        weights = jnp.where(allowed, jnp.exp(scores - new_top[..., None, None]), 0.0)
        total_new = jnp.sum(weights, axis=(3, 4))
        mixed = jnp.einsum(
            "shqgk,gskhd->shqd",
            weights.astype(jnp.bfloat16),
            values_split,
            preferred_element_type=jnp.float32,
        )
        top_run = new_top
        attended = (
            (mixed / total_new[..., None])
            .transpose(0, 2, 1, 3)
            .reshape(row_count, head_local * head_dim)
            .astype(jnp.bfloat16)
        )
        out_layer = out_weight[layer_idx]
        fc1_layer = fc1_weight[layer_idx]
        fc2_layer = fc2_weight[layer_idx]
        fc1_layer_bias = fc1_bias[layer_idx]
        own_rows = lax.dynamic_slice_in_dim(full_in, tensor_pos * share_rows, share_rows, 0).astype(
            jnp.float32
        )
        first = (
            own_rows
            + lax.psum_scatter(
                jnp.dot(attended, out_layer, preferred_element_type=jnp.float32).astype(
                    jnp.bfloat16
                ),
                "tensor",
                scatter_dimension=0,
                tiled=True,
            ).astype(jnp.float32)
            + out_bias[layer_idx]
        )
        normed_two = layer_norm(first, ln2_gain[layer_idx], ln2_bias[layer_idx]).astype(
            jnp.bfloat16
        )
        inner = jax.nn.gelu(
            jnp.dot(
                lax.all_gather(normed_two, "tensor", axis=0, tiled=True),
                fc1_layer,
                preferred_element_type=jnp.float32,
            )
            + fc1_layer_bias,
            approximate=False,
        ).astype(jnp.bfloat16)
        mlp_share = lax.psum_scatter(
            jnp.dot(inner, fc2_layer, preferred_element_type=jnp.float32).astype(jnp.bfloat16),
            "tensor",
            scatter_dimension=0,
            tiled=True,
        ).astype(jnp.float32)
        new_share = (first + mlp_share + fc2_bias[layer_idx]).astype(jnp.bfloat16)
        if layer_idx + 1 < LAYERS:
            full_in = lax.all_gather(new_share, "tensor", axis=0, tiled=True)
    return new_share[None]


def shards_clip(
    frames_in,
    frame_time,
    cond_count,
    ln1_gain,
    ln1_bias,
    qkv_weight,
    qkv_bias,
    out_weight,
    out_bias,
    ln2_gain,
    ln2_bias,
    fc1_weight,
    fc1_bias,
    fc2_weight,
    fc2_bias,
):
    frame_count = frame_time.shape[0]
    piece_count = lax.axis_size("tm")
    frame_split = piece_count // frame_count
    piece_rows = PATCH_DEV + COND // frame_split
    row_count = frames_in.shape[1]
    seq_count = row_count // piece_rows
    clips = seq_count // piece_count
    head_dim = D // HEADS
    head_local = qkv_weight.shape[3] // head_dim
    scale = head_dim ** (-0.5)
    tensor_size = lax.axis_size("tensor")
    tensor_pos = lax.axis_index("tensor")
    share_rows = row_count // tensor_size
    share_cols = D // tensor_size
    piece_time, valid = piece_tables(frame_time, cond_count, piece_count, frame_split, piece_rows)
    row_time = jnp.repeat(piece_time, piece_rows)
    allowed = (row_time[None, :] <= row_time[:, None]) & valid.reshape(1, -1)
    clip_rows = piece_count * piece_rows
    mine = lax.dynamic_slice_in_dim(frames_in[0], tensor_pos * share_cols, share_cols, 1)
    mine = mine.reshape(piece_count, clips, piece_rows, share_cols)
    mine = lax.all_to_all(mine, "tm", 0, 0, tiled=True)
    mine = mine.transpose(1, 0, 2, 3).reshape(row_count, share_cols)
    full_in = lax.all_gather(mine, "tensor", axis=1, tiled=True)
    new_share = None
    for layer_idx in range(LAYERS):
        normed = layer_norm(
            full_in.astype(jnp.float32), ln1_gain[layer_idx], ln1_bias[layer_idx]
        ).astype(jnp.bfloat16)
        parts = []
        for i in range(3):
            part = jnp.dot(normed, qkv_weight[layer_idx, i], preferred_element_type=jnp.float32)
            part = (part + qkv_bias[layer_idx, i]).astype(jnp.bfloat16)
            parts.append(part.reshape(clips, clip_rows, head_local, head_dim))
        queries, keys, values = parts
        scores = (
            jnp.einsum("sqhd,skhd->shqk", queries, keys, preferred_element_type=jnp.float32) * scale
        )
        scores = jnp.where(allowed, scores, -1e30)
        top = jnp.max(scores, axis=-1, keepdims=True)
        weights = jnp.where(allowed, jnp.exp(scores - top), 0.0)
        total = jnp.sum(weights, axis=-1, keepdims=True)
        mixed = jnp.einsum(
            "shqk,skhd->shqd",
            weights.astype(jnp.bfloat16),
            values,
            preferred_element_type=jnp.float32,
        )
        attended = (
            (mixed / total)
            .transpose(0, 2, 1, 3)
            .reshape(row_count, head_local * head_dim)
            .astype(jnp.bfloat16)
        )
        own_rows = lax.dynamic_slice_in_dim(full_in, tensor_pos * share_rows, share_rows, 0).astype(
            jnp.float32
        )
        first = (
            own_rows
            + lax.psum_scatter(
                jnp.dot(attended, out_weight[layer_idx], preferred_element_type=jnp.float32).astype(
                    jnp.bfloat16
                ),
                "tensor",
                scatter_dimension=0,
                tiled=True,
            ).astype(jnp.float32)
            + out_bias[layer_idx]
        )
        normed_two = layer_norm(first, ln2_gain[layer_idx], ln2_bias[layer_idx]).astype(
            jnp.bfloat16
        )
        inner = jax.nn.gelu(
            jnp.dot(
                lax.all_gather(normed_two, "tensor", axis=0, tiled=True),
                fc1_weight[layer_idx],
                preferred_element_type=jnp.float32,
            )
            + fc1_bias[layer_idx],
            approximate=False,
        ).astype(jnp.bfloat16)
        mlp_share = lax.psum_scatter(
            jnp.dot(inner, fc2_weight[layer_idx], preferred_element_type=jnp.float32).astype(
                jnp.bfloat16
            ),
            "tensor",
            scatter_dimension=0,
            tiled=True,
        ).astype(jnp.float32)
        new_share = (first + mlp_share + fc2_bias[layer_idx]).astype(jnp.bfloat16)
        if layer_idx + 1 < LAYERS:
            full_in = lax.all_gather(new_share, "tensor", axis=0, tiled=True)
    cols = jnp.stack(jnp.split(new_share, tensor_size, axis=1))
    cols = lax.all_to_all(cols, "tensor", 0, 0, tiled=True)
    cols = cols.reshape(clips, piece_count, piece_rows, share_cols).transpose(1, 0, 2, 3)
    cols = lax.all_to_all(cols, "tm", 0, 0, tiled=True)
    cols = cols.reshape(tensor_size, share_rows, share_cols)
    cols = lax.all_to_all(cols, "tensor", 0, 0, tiled=True)
    out = cols.transpose(1, 0, 2).reshape(share_rows, D)
    return out[None]


def shards(frames_in, frame_time, cond_count, *rest):
    frame_split = lax.axis_size("tm") // frame_time.shape[0]
    piece_rows = PATCH_DEV + COND // frame_split
    seq_count = frames_in.shape[1] // piece_rows
    by_clip = seq_count % lax.axis_size("tm") == 0
    body = shards_clip if by_clip else shards_gather
    return body(frames_in, frame_time, cond_count, *rest)


def solution(mesh):
    in_specs = (
        P("tm", None, None),
        P(),
        P(),
        P(),
        P(),
        P(None, None, None, "tensor"),
        P(None, None, "tensor"),
        P(None, "tensor", None),
        P(),
        P(),
        P(),
        P(None, None, "tensor"),
        P(None, "tensor"),
        P(None, "tensor", None),
        P(),
    )
    out_specs = P("tm", "tensor", None)
    return jax.shard_map(shards, mesh=mesh, in_specs=in_specs, out_specs=out_specs, check_vma=False)
```

profile of v0, /device:TPU:0, one launch (start us, length us, event | category | flops | bytes accessed | tf_op | source)
XLA Modules:
  0.0 282.2 jit_solution(10008635543005344850)
XLA Ops:
  6.6 1.2 copy-done
  7.8 0.8 reshape.180
  8.6 7.3 %all-to-all-start = ((bf16[8,1,66,256]{3,2,1,0:T(8,128)(2,1)}), bf16[8,1,66,256]{3,2,1,0:T(8,128)(2,1)S(1)}, u32[]{:S(2)}, u32[]{:S(2)}) async-start(bf16[8,1,66,256]{3,2,1,0:T(8,128)(2,1)} %bitcast), calls=%async_computation | async-start | bytes 589824 | tf_op jit(solution)/shard_map/all_to_all | solution.py:192
  15.9 0.8 select_reduce_fusion.1
  16.7 0.8 select_reduce_fusion
  17.5 8.0 %all-to-all-done = bf16[8,1,66,256]{3,2,1,0:T(8,128)(2,1)S(1)} async-done(((bf16[8,1,66,256]{3,2,1,0:T(8,128)(2,1)}), bf16[8,1,66,256]{3,2,1,0:T(8,128)(2,1)S(1)}, u32[]{:S(2)}, u32[]{:S(2)}) %all-to-all-start) | async-done | bytes 270368 | tf_op jit(solution)/shard_map/all_to_all | solution.py:192
  25.5 0.8 reshape_transpose.3
  26.7 0.6 fusion.255
  27.3 0.6 fusion.253
  27.9 0.6 fusion.252
  28.5 0.6 fusion.250
  29.1 0.6 fusion.249
  29.7 1.0 compare_and_fusion
  30.8 11.8 %all-gather.8.cloned.1.call-done = bf16[528,1024]{1,0:T(8,128)(2,1)} async-done(((bf16[528,256]{1,0:T(8,128)(2,1)}), bf16[528,1024]{1,0:T(8,128)(2,1)}) %all-gather.8.cloned.1.call-update) | async-done | bytes 1081360 | tf_op jit(solution)/shard_map/all_gather | solution.py:194
  42.5 1.6 convert_reduce_fusion.1
  44.1 1.7 fusion.26
  45.8 0.5 fusion.29
  46.2 1.5 fusion.82
  47.7 0.9 copy.56
  48.7 1.5 fusion.80
  50.2 0.9 copy.54
  51.0 1.5 fusion.81
  52.8 5.4 %fusion.256 = (f32[4,528]{1,0:T(4,128)S(1)}, bf16[4,528,528]{1,2,0:T(8,128)(2,1)}) fusion(pred[528,528]{0,1:T(8,128)(4,1)} %compare_and_fusion, bf16[528,4,64]{0,2,1:T(8,128)(2,1)} %bitcast.137, bf16[528,4,64]{0,2,1:T(8,128)(2,1)S(1)} %bitcast.139), kind=kOutput, calls=%fused_computation.290 | convolution fusion | flops 149428752 | bytes 3058176 | tf_op jit(solution)/shard_map/sub | solution.py:211
  58.2 2.5 fusion.77
  60.7 0.5 convolution_convert_fusion.1
  61.2 15.4 %fusion = bf16[136,1024]{1,0:T(8,128)(2,1)S(1)} fusion(bf16[528,1024]{1,0:T(8,128)(2,1)S(1)} %convolution_convert_fusion.1), kind=kCustom, calls=%all-reduce-scatter | all-reduce-scatter fusion | flops 557057 | bytes 1360384
  76.6 1.3 collective-permute-start
  77.9 0.6 fusion.251
  78.5 0.6 dynamic-slice.11
  80.7 1.1 fusion.180
  82.0 0.6 fusion.254
  82.6 18.1 %all-gather.10.cloned.1.call-done = bf16[4,132,1024]{2,1,0:T(8,128)(2,1)} async-done(((bf16[1,132,1024]{2,1,0:T(8,128)(2,1)}), bf16[4,132,1024]{2,1,0:T(8,128)(2,1)}) %all-gather.10.cloned.1.call-update) | async-done | bytes 1081360 | tf_op jit(solution)/shard_map/all_gather | solution.py:245
  100.7 1.3 reshape.189
  102.1 9.7 %fusion.62 = bf16[528,1024]{1,0:T(8,128)(2,1)} fusion(bf16[2,1024,1024]{2,1,0:T(8,128)(2,1)} %param.28, f32[1024]{0:T(1024)} %bitcast.161, bf16[528,1024]{1,0:T(8,128)(2,1)S(1)} %reshape.189, bf16[2,1024,1024]{2,1,0:T(8,128)(2,1)} %param.26), kind=kOutput, calls=%fused_computation.84 | convolution fusion | flops 2250817536 | bytes 6361088 | tf_op jit(solution)/shard_map/dot_general | solution.py:253
  111.8 15.9 %fusion.1 = bf16[136,1024]{1,0:T(8,128)(2,1)S(1)} fusion(bf16[528,1024]{1,0:T(8,128)(2,1)} %fusion.62), kind=kCustom, calls=%all-reduce-scatter.1 | all-reduce-scatter fusion | flops 557057 | bytes 1360384
  127.7 1.3 collective-permute-start.1
  129.0 1.4 fusion.248
  130.7 1.6 fusion.181
  132.7 19.2 %all-gather.12.cloned.1.call-done = bf16[4,132,1024]{2,1,0:T(8,128)(2,1)} async-done(((bf16[1,132,1024]{2,1,0:T(8,128)(2,1)}), bf16[4,132,1024]{2,1,0:T(8,128)(2,1)}) %all-gather.12.cloned.1.call-update) | async-done | bytes 1081360 | tf_op jit(solution)/shard_map/all_gather | solution.py:262
  151.9 1.3 reshape.191
  154.0 0.5 fusion.25
  154.5 1.5 fusion.85
  156.0 0.9 copy.60
  156.9 1.5 fusion.83
  158.4 0.9 copy.58
  159.3 1.5 fusion.84
  161.0 5.4 %fusion.257 = (f32[4,528]{1,0:T(4,128)S(1)}, bf16[4,528,528]{1,2,0:T(8,128)(2,1)}) fusion(pred[528,528]{0,1:T(8,128)(4,1)} %compare_and_fusion, bf16[528,4,64]{0,2,1:T(8,128)(2,1)} %bitcast.136, bf16[528,4,64]{0,2,1:T(8,128)(2,1)S(1)} %bitcast.138), kind=kOutput, calls=%fused_computation.291 | convolution fusion | flops 149428752 | bytes 3058176 | tf_op jit(solution)/shard_map/sub | solution.py:211
  166.4 2.5 fusion.74
  169.0 0.5 convolution_convert_fusion
  169.4 15.4 %fusion.2 = bf16[136,1024]{1,0:T(8,128)(2,1)S(1)} fusion(bf16[528,1024]{1,0:T(8,128)(2,1)S(1)} %convolution_convert_fusion), kind=kCustom, calls=%all-reduce-scatter.2 | all-reduce-scatter fusion | flops 557057 | bytes 1360384
  184.8 1.6 collective-permute-start.2
  186.4 0.6 collective-permute-done.2
  187.9 1.1 fusion.182
  189.0 20.0 %all-gather.14.cloned.1.call-done = bf16[4,132,1024]{2,1,0:T(8,128)(2,1)} async-done(((bf16[1,132,1024]{2,1,0:T(8,128)(2,1)}), bf16[4,132,1024]{2,1,0:T(8,128)(2,1)}) %all-gather.14.cloned.1.call-update) | async-done | bytes 1081360 | tf_op jit(solution)/shard_map/all_gather | solution.py:245
  209.0 1.3 reshape.193
  210.3 9.7 %fusion.65 = bf16[528,1024]{1,0:T(8,128)(2,1)} fusion(bf16[2,1024,1024]{2,1,0:T(8,128)(2,1)} %param.28, f32[1024]{0:T(1024)} %bitcast.160, bf16[528,1024]{1,0:T(8,128)(2,1)S(1)} %reshape.193, bf16[2,1024,1024]{2,1,0:T(8,128)(2,1)} %param.26), kind=kOutput, calls=%fused_computation.85 | convolution fusion | flops 2250817536 | bytes 6361088 | tf_op jit(solution)/shard_map/dot_general | solution.py:253
  220.1 15.9 %fusion.3 = bf16[136,1024]{1,0:T(8,128)(2,1)S(1)} fusion(bf16[528,1024]{1,0:T(8,128)(2,1)} %fusion.65), kind=kCustom, calls=%all-reduce-scatter.3 | all-reduce-scatter fusion | flops 557057 | bytes 1360384
  236.0 1.3 collective-permute-start.3
  237.3 0.8 collective-permute-done.3
  238.5 0.9 add_convert_fusion
  239.5 10.7 %all_to_all.20 = bf16[4,132,256]{2,1,0:T(8,128)(2,1)S(1)} all-to-all(bf16[4,132,256]{2,1,0:T(8,128)(2,1)S(1)} %pad_maximum_fusion), channel_id=1, replica_groups=mesh['tm'=8,'tensor'=4] {'tensor'}, dimensions={0} | all-to-all | bytes 540672 | tf_op jit(solution)/shard_map/all_to_all | solution.py:264
  250.2 15.8 %all_to_all.21 = bf16[8,1,66,256]{3,2,1,0:T(8,128)(2,1)S(1)} all-to-all(bf16[8,1,66,256]{3,2,1,0:T(8,128)(2,1)S(1)} %bitcast.132), channel_id=1, replica_groups=mesh['tm'=8,'tensor'=4] {'tm'}, dimensions={0} | all-to-all | bytes 540672 | tf_op jit(solution)/shard_map/all_to_all | solution.py:266
  266.1 8.5 %all_to_all.22 = bf16[4,132,256]{2,1,0:T(8,128)(2,1)S(1)} all-to-all(bf16[4,132,256]{2,1,0:T(8,128)(2,1)S(1)} %reshape.187), channel_id=1, replica_groups=mesh['tm'=8,'tensor'=4] {'tensor'}, dimensions={0} | all-to-all | bytes 540672 | tf_op jit(solution)/shard_map/all_to_all | solution.py:268
  274.7 0.9 broadcast_in_dim_reshape.2
  (90 shorter events, 5.0 us)
Async XLA Ops:
  6.5 1.2 copy-start
  6.5 20.2 %copy-start.18 = (f32[2,3,256]{2,0,1:T(2,128)S(1)}, f32[2,3,256]{2,0,1:T(2,128)}, u32[]{:S(2)}) copy-start(f32[2,3,256]{2,0,1:T(2,128)} %param.21) | copy-start | bytes 18436
  6.5 20.8 %copy-start.12 = (f32[2,1024]{1,0:T(2,128)S(1)}, f32[2,1024]{1,0:T(2,128)}, u32[]{:S(2)}) copy-start(f32[2,1024]{1,0:T(2,128)} %param.25) | copy-start | bytes 24580
  6.5 21.4 %copy-start.13 = (f32[2,1024]{1,0:T(2,128)S(1)}, f32[2,1024]{1,0:T(2,128)}, u32[]{:S(2)}) copy-start(f32[2,1024]{1,0:T(2,128)} %param.24) | copy-start | bytes 24580
  6.5 22.0 %copy-start.14 = (f32[2,1024]{1,0:T(2,128)S(1)}, f32[2,1024]{1,0:T(2,128)}, u32[]{:S(2)}) copy-start(f32[2,1024]{1,0:T(2,128)} %param.19) | copy-start | bytes 24580
  6.5 22.6 %copy-start.15 = (f32[2,1024]{1,0:T(2,128)S(1)}, f32[2,1024]{1,0:T(2,128)}, u32[]{:S(2)}) copy-start(f32[2,1024]{1,0:T(2,128)} %param.18) | copy-start | bytes 24580
  8.6 16.9 %all-to-all-start = ((bf16[8,1,66,256]{3,2,1,0:T(8,128)(2,1)}), bf16[8,1,66,256]{3,2,1,0:T(8,128)(2,1)S(1)}, u32[]{:S(2)}, u32[]{:S(2)}) async-start(bf16[8,1,66,256]{3,2,1,0:T(8,128)(2,1)} %bitcast), calls=%async_computation | async-start | bytes 589824 | tf_op jit(solution)/shard_map/all_to_all | solution.py:192
  15.9 26.6 %all-gather.8.cloned.1.call-start = ((), (), s32[]{:S(2)}) async-start(), calls=%async_computation.4 | async-start | bytes 1351680 | tf_op jit(solution)/shard_map/all_gather | solution.py:194
  26.3 74.4 %all-gather.10.cloned.1.call-start = ((), (), s32[]{:S(2)}) async-start(), calls=%async_computation.5 | async-start | bytes 1392640 | tf_op jit(solution)/shard_map/all_gather | solution.py:245
  42.5 3.3 %copy-start.1 = (bf16[528,1024]{1,0:T(8,128)(2,1)S(1)}, bf16[528,1024]{1,0:T(8,128)(2,1)}, u32[]{:S(2)}) copy-start(bf16[528,1024]{1,0:T(8,128)(2,1)} %all-gather.8.cloned.1.call-done) | copy-start | bytes 3244036
  52.7 5.4 %copy-start.5 = (bf16[528,256]{0,1:T(8,128)(2,1)S(1)}, bf16[528,256]{0,1:T(8,128)(2,1)}, u32[]{:S(2)}) copy-start(bf16[528,256]{0,1:T(8,128)(2,1)} %copy.56) | copy-start | bytes 811012
  58.2 2.5 copy-start.2
  60.7 17.2 %copy-start.16 = (f32[2,1024]{1,0:T(2,128)S(1)}, f32[2,1024]{1,0:T(2,128)}, u32[]{:S(2)}) copy-start(f32[2,1024]{1,0:T(2,128)} %param.23) | copy-start | bytes 24580
  60.7 17.8 %copy-start.22 = (u32[32]{0:T(128)S(1)}, u32[32]{0:T(128)}, u32[]{:S(2)}) copy-start(u32[32]{0:T(128)} %constant.128) | copy-start | bytes 388
  61.2 20.8 %copy-start.17 = (f32[2,1024]{1,0:T(2,128)S(1)}, f32[2,1024]{1,0:T(2,128)}, u32[]{:S(2)}) copy-start(f32[2,1024]{1,0:T(2,128)} %param.27) | copy-start | bytes 24580
  76.6 3.1 %collective-permute-start = (bf16[12,1024]{1,0:T(8,128)(2,1)S(1)}, bf16[12,1024]{1,0:T(8,128)(2,1)S(1)}, u32[]{:S(2)}, u32[]{:S(2)}) collective-permute-start(bf16[12,1024]{1,0:T(8,128)(2,1)S(1)} %slice.128), channel_id=1, source_target_pairs={{0,1},{1,2},{2,3},{4,5},{5,6},{6,7},{8,9},{9,10},{10,11},{12,13},{... | collective-permute-start | bytes 73736
  78.5 4.1 %copy-start.7 = (f32[1,1024]{1,0:T(1,128)}, f32[1,1024]{1,0:T(1,128)S(1)}, u32[]{:S(2)}) copy-start(f32[1,1024]{1,0:T(1,128)S(1)} %get-tuple-element.15) | copy-start | bytes 12292
  81.8 70.1 %all-gather.12.cloned.1.call-start = ((), (), s32[]{:S(2)}) async-start(), calls=%async_computation.6 | async-start | bytes 1392640 | tf_op jit(solution)/shard_map/all_gather | solution.py:262
  127.7 2.7 collective-permute-start.1
  132.4 21.6 %copy-start.10 = (f32[1,1024]{1,0:T(1,128)S(1)}, f32[1,1024]{1,0:T(1,128)}, u32[]{:S(2)}) copy-start(f32[1,1024]{1,0:T(1,128)} %get-tuple-element.13) | copy-start | bytes 12292
  132.4 21.6 %copy-start.11 = (f32[1,1024]{1,0:T(1,128)S(1)}, f32[1,1024]{1,0:T(1,128)}, u32[]{:S(2)}) copy-start(f32[1,1024]{1,0:T(1,128)} %get-tuple-element.11) | copy-start | bytes 12292
  132.4 76.6 %all-gather.14.cloned.1.call-start = ((), (), s32[]{:S(2)}) async-start(), calls=%async_computation.7 | async-start | bytes 1392640 | tf_op jit(solution)/shard_map/all_gather | solution.py:245
  153.3 1.2 copy-start.21
  154.0 2.9 %copy-start.20 = (f32[1,1,256]{2,0,1:T(1,128)S(1)}, f32[1,1,256]{2,0,1:T(1,128)}, u32[]{:S(2)}) copy-start(f32[1,1,256]{2,0,1:T(1,128)} %get-tuple-element.24) | copy-start | bytes 3076
  156.0 3.3 %copy-start.19 = (f32[1,1,256]{2,0,1:T(1,128)S(1)}, f32[1,1,256]{2,0,1:T(1,128)}, u32[]{:S(2)}) copy-start(f32[1,1,256]{2,0,1:T(1,128)} %get-tuple-element.23) | copy-start | bytes 3076
  161.0 5.4 %copy-start.4 = (bf16[528,256]{0,1:T(8,128)(2,1)S(1)}, bf16[528,256]{0,1:T(8,128)(2,1)}, u32[]{:S(2)}) copy-start(bf16[528,256]{0,1:T(8,128)(2,1)} %copy.60) | copy-start | bytes 811012
  166.4 2.5 copy-start.3
  168.9 18.4 %copy-start.6 = (f32[1,1024]{1,0:T(1,128)S(1)}, f32[1,1024]{1,0:T(1,128)}, u32[]{:S(2)}) copy-start(f32[1,1024]{1,0:T(1,128)} %get-tuple-element.16) | copy-start | bytes 12292
  169.0 18.9 %copy-start.8 = (f32[1,1024]{1,0:T(1,128)S(1)}, f32[1,1024]{1,0:T(1,128)}, u32[]{:S(2)}) copy-start(f32[1,1024]{1,0:T(1,128)} %get-tuple-element.20) | copy-start | bytes 12292
  169.0 18.9 %copy-start.9 = (f32[1,1024]{1,0:T(1,128)S(1)}, f32[1,1024]{1,0:T(1,128)}, u32[]{:S(2)}) copy-start(f32[1,1024]{1,0:T(1,128)} %get-tuple-element.18) | copy-start | bytes 12292
  184.8 2.1 collective-permute-start.2
  236.0 2.1 collective-permute-start.3
Sparse Core Ops, SparseCore 0:
  26.4 16.0 all-gather.7
  81.9 18.7 all-gather.9
  132.5 19.3 all-gather.11
  189.1 19.8 all-gather.13
where the time goes:
time: 283 us; the launch traced here: 282 us
  blocking collectives  97.6 us (34%)
  waiting for transfers between devices  78.6 us (28%)
  matrix products  45.1 us (16%)
  local copies, waits for them, and re-layouts  19.8 us (7%)
  between operations  14.3 us (5%)
  other arithmetic  13.4 us (5%)
  starting transfers between devices  13.3 us (5%)
    unnamed x4, blocking collectives  62.5 us
    all_gather x2, waiting for transfers between devices, shards_clip(): lax.all_gather(normed_two, 'tensor', axis=0, tiled=True)  38.1 us
    dot_general x2, matrix products, shards_clip(): jnp.dot(inner, fc2_weight[layer_idx], preferred_element_type=jnp.float32)  19.5 us
    all_gather x1, waiting for transfers between devices, shards_clip(): full_in = lax.all_gather(new_share, 'tensor', axis=0, tiled=True)  19.2 us
    all_to_all x2, blocking collectives, shards_clip(): cols = lax.all_to_all(cols, 'tensor', 0, 0, tiled=True)  19.2 us
    all_to_all x1, blocking collectives, shards_clip(): cols = lax.all_to_all(cols, 'tm', 0, 0, tiled=True)  15.8 us
    all_gather x1, waiting for transfers between devices, shards_clip(): full_in = lax.all_gather(mine, 'tensor', axis=1, tiled=True)  11.8 us
    sub x2, matrix products, shards_clip(): weights = jnp.where(allowed, jnp.exp(scores - top), 0.0)  10.8 us
  transfers between devices with their start and end apart: 9, of which 7 were waited for; matrix products, arithmetic and copies ran while one was open for 3% of the time, Pallas kernels for 0%

commit v1 on v0

--- a/solution.py
+++ b/solution.py
@@ -8,6 +8,35 @@
 PATCH_DEV = 64
 COND = 2
 LAYERS = 2
+
+
+def recover_regions(m, dim_no):
+    fresh = list(m.shape[1:])
+    fresh[dim_no] *= m.shape[0]
+    frame_out = jnp.moveaxis(m, 0, dim_no).reshape(fresh)
+    return frame_out
+
+
+def test_table(target, which_axis):
+    odd = lax.axis_size(which_axis)
+    field_out = lax.axis_index(which_axis)
+    carry_out, built = (odd, field_out)
+    local_part, r_now = (target[None], 1)
+    while r_now < carry_out:
+        placed = tuple(((kk, kk ^ r_now) for kk in range(carry_out)))
+        newest = lax.ppermute(local_part, which_axis, placed)
+        h_now = built & r_now == 0
+        tmp = jnp.where(h_now, local_part, newest)
+        local_out = jnp.where(h_now, newest, local_part)
+        local_part = jnp.concatenate([tmp, local_out])
+        r_now *= 2
+    return local_part
+
+
+def loops_register(slab_in, view, array_dim):
+    mid_arr = test_table(slab_in, view)
+    item_now = recover_regions(mid_arr, array_dim)
+    return item_now
 
 
 def layer_norm(inputs, gain_row, bias_row):
@@ -242,7 +271,7 @@
         )
         inner = jax.nn.gelu(
             jnp.dot(
-                lax.all_gather(normed_two, "tensor", axis=0, tiled=True),
+                loops_register(normed_two, "tensor", 0),
                 fc1_weight[layer_idx],
                 preferred_element_type=jnp.float32,
             )

time: 283 us -> 285 us (level)
  waiting for transfers between devices: 78.6 us -> 68.6 us
  starting transfers between devices: 13.3 us -> 19.6 us
  other arithmetic: 13.4 us -> 16.9 us
    all_gather x2 -> x0, waiting for transfers between devices: 38.1 us -> none  [shards_clip(): lax.all_gather(normed_two, 'tensor', axis=0, tiled=True)]
    ppermute x0 -> x4, waiting for transfers between devices: none -> 27.8 us  [test_table(): newest = lax.ppermute(local_part, which_axis, placed)]
    ppermute x0 -> x4, starting transfers between devices: none -> 6.4 us  [test_table(): newest = lax.ppermute(local_part, which_axis, placed)]
    unnamed x58 -> x56, local copies, waits for them, and re-layouts: 7.26 us -> 4.57 us
  transfers between devices with their start and end apart: 9 -> 11, of which waited for: 7 -> 9; matrix products, arithmetic and copies ran while one was open for 3% -> 3% of each run, Pallas kernels for 0% -> 0%
where the time goes in v1:
time: 285 us; the launch traced here: 284 us
  blocking collectives  97.5 us (34%)
  waiting for transfers between devices  68.6 us (24%)
  matrix products  45.1 us (16%)
  local copies, waits for them, and re-layouts  21.7 us (8%)
  starting transfers between devices  19.6 us (7%)
  other arithmetic  16.9 us (6%)
  between operations  14.6 us (5%)
    unnamed x4, blocking collectives  62.3 us
    ppermute x4, waiting for transfers between devices, test_table(): newest = lax.ppermute(local_part, which_axis, placed)  27.8 us
    all_gather x1, waiting for transfers between devices, shards_clip(): full_in = lax.all_gather(new_share, 'tensor', axis=0, tiled=True)  19.5 us
    dot_general x2, matrix products, shards_clip(): jnp.dot(inner, fc2_weight[layer_idx], preferred_element_type=jnp.float32)  19.4 us
    all_to_all x2, blocking collectives, shards_clip(): cols = lax.all_to_all(cols, 'tensor', 0, 0, tiled=True)  19.4 us
    all_to_all x1, blocking collectives, shards_clip(): cols = lax.all_to_all(cols, 'tm', 0, 0, tiled=True)  15.8 us
    all_gather x1, waiting for transfers between devices, shards_clip(): full_in = lax.all_gather(mine, 'tensor', axis=1, tiled=True)  11.8 us
    sub x2, matrix products, shards_clip(): weights = jnp.where(allowed, jnp.exp(scores - top), 0.0)  10.9 us
  transfers between devices with their start and end apart: 11, of which 9 were waited for; matrix products, arithmetic and copies ran while one was open for 3% of the time, Pallas kernels for 0%

profile of v1, /device:TPU:0, one launch (start us, length us, event | category | flops | bytes accessed | tf_op | source)
XLA Modules:
  0.0 284.2 jit_solution(14161163533253484040)
XLA Ops:
  6.6 1.2 copy-done
  7.8 0.8 reshape.186
  8.6 7.3 %all-to-all-start = ((bf16[8,1,66,256]{3,2,1,0:T(8,128)(2,1)}), bf16[8,1,66,256]{3,2,1,0:T(8,128)(2,1)S(1)}, u32[]{:S(2)}, u32[]{:S(2)}) async-start(bf16[8,1,66,256]{3,2,1,0:T(8,128)(2,1)} %bitcast), calls=%async_computation | async-start | bytes 589824 | tf_op jit(solution)/shard_map/all_to_all | solution.py:221
  15.9 0.8 select_reduce_fusion.1
  16.7 0.8 select_reduce_fusion
  17.5 8.0 %all-to-all-done = bf16[8,1,66,256]{3,2,1,0:T(8,128)(2,1)S(1)} async-done(((bf16[8,1,66,256]{3,2,1,0:T(8,128)(2,1)}), bf16[8,1,66,256]{3,2,1,0:T(8,128)(2,1)S(1)}, u32[]{:S(2)}, u32[]{:S(2)}) %all-to-all-start) | async-done | bytes 270368 | tf_op jit(solution)/shard_map/all_to_all | solution.py:221
  25.5 0.8 reshape_transpose.3
  26.7 0.6 fusion.255
  27.3 0.6 fusion.253
  28.5 0.6 fusion.250
  29.1 0.6 fusion.249
  29.7 1.0 compare_and_fusion
  30.7 11.8 %all-gather.4.cloned.1.call-done = bf16[528,1024]{1,0:T(8,128)(2,1)} async-done(((bf16[528,256]{1,0:T(8,128)(2,1)}), bf16[528,1024]{1,0:T(8,128)(2,1)}) %all-gather.4.cloned.1.call-update) | async-done | bytes 1081360 | tf_op jit(solution)/shard_map/all_gather | solution.py:223
  42.5 1.6 convert_reduce_fusion.1
  44.1 1.7 fusion.26
  46.2 1.5 fusion.82
  47.7 0.9 copy.62
  48.7 1.5 fusion.80
  50.1 0.9 copy.60
  51.1 1.5 fusion.81
  52.8 5.4 %fusion.256 = (f32[4,528]{1,0:T(4,128)S(1)}, bf16[4,528,528]{1,2,0:T(8,128)(2,1)}) fusion(pred[528,528]{0,1:T(8,128)(4,1)} %compare_and_fusion, bf16[528,4,64]{0,2,1:T(8,128)(2,1)} %bitcast.137, bf16[528,4,64]{0,2,1:T(8,128)(2,1)S(1)} %bitcast.139), kind=kOutput, calls=%fused_computation.302 | convolution fusion | flops 149428752 | bytes 3058176 | tf_op jit(solution)/shard_map/sub | solution.py:240
  58.2 2.5 fusion.77
  61.2 15.4 %fusion = bf16[136,1024]{1,0:T(8,128)(2,1)S(1)} fusion(bf16[528,1024]{1,0:T(8,128)(2,1)S(1)} %convolution_convert_fusion.1), kind=kCustom, calls=%all-reduce-scatter | all-reduce-scatter fusion | flops 557057 | bytes 1360384
  76.6 1.5 collective-permute-start.4
  81.3 1.1 collective-permute-start
  82.3 1.3 collective-permute-done
  83.6 1.0 broadcast_select_fusion.7
  84.7 1.3 copy.64
  86.0 1.5 collective-permute-start.1
  88.1 12.8 %collective-permute-done.1 = bf16[2,132,1024]{2,0,1:T(2,128)(2,1)} collective-permute-done((bf16[2,132,1024]{2,0,1:T(2,128)(2,1)}, bf16[2,132,1024]{2,0,1:T(2,128)(2,1)}, u32[]{:S(2)}, u32[]{:S(2)}) %collective-permute-start.1) | collective-permute-done | bytes 540704 | tf_op jit(solution)/shard_map/ppermute | solution.py:27
  100.9 1.3 broadcast_select_fusion.3
  102.2 1.1 pad_maximum_fusion
  103.3 1.3 reshape.190
  104.6 9.7 %fusion.62 = bf16[528,1024]{1,0:T(8,128)(2,1)} fusion(bf16[2,1024,1024]{2,1,0:T(8,128)(2,1)} %param.28, f32[1024]{0:T(1024)} %bitcast.161, bf16[528,1024]{1,0:T(8,128)(2,1)S(1)} %reshape.190, bf16[2,1024,1024]{2,1,0:T(8,128)(2,1)} %param.26), kind=kOutput, calls=%fused_computation.84 | convolution fusion | flops 2250817536 | bytes 6361088 | tf_op jit(solution)/shard_map/dot_general | solution.py:282
  114.4 15.5 %fusion.1 = bf16[136,1024]{1,0:T(8,128)(2,1)S(1)} fusion(bf16[528,1024]{1,0:T(8,128)(2,1)} %fusion.62), kind=kCustom, calls=%all-reduce-scatter.1 | all-reduce-scatter fusion | flops 557057 | bytes 1360384
  129.9 1.5 collective-permute-start.5
  131.4 1.4 fusion.248
  133.2 1.7 fusion.181
  134.9 19.5 %all-gather.6.cloned.1.call-done = bf16[4,132,1024]{2,1,0:T(8,128)(2,1)} async-done(((bf16[1,132,1024]{2,1,0:T(8,128)(2,1)}), bf16[4,132,1024]{2,1,0:T(8,128)(2,1)}) %all-gather.6.cloned.1.call-update) | async-done | bytes 1081360 | tf_op jit(solution)/shard_map/all_gather | solution.py:291
  154.4 1.3 reshape.197
  156.9 1.5 fusion.85
  158.4 0.9 copy.69
  159.4 1.5 fusion.83
  160.8 0.9 copy.67
  161.8 1.5 fusion.84
  163.5 5.4 %fusion.257 = (f32[4,528]{1,0:T(4,128)S(1)}, bf16[4,528,528]{1,2,0:T(8,128)(2,1)}) fusion(pred[528,528]{0,1:T(8,128)(4,1)} %compare_and_fusion, bf16[528,4,64]{0,2,1:T(8,128)(2,1)} %bitcast.136, bf16[528,4,64]{0,2,1:T(8,128)(2,1)S(1)} %bitcast.138), kind=kOutput, calls=%fused_computation.303 | convolution fusion | flops 149428752 | bytes 3058176 | tf_op jit(solution)/shard_map/sub | solution.py:240
  168.9 2.5 fusion.74
  171.9 15.4 %fusion.2 = bf16[136,1024]{1,0:T(8,128)(2,1)S(1)} fusion(bf16[528,1024]{1,0:T(8,128)(2,1)S(1)} %convolution_convert_fusion), kind=kCustom, calls=%all-reduce-scatter.2 | all-reduce-scatter fusion | flops 557057 | bytes 1360384
  187.3 1.6 collective-permute-start.6
  190.8 1.2 collective-permute-start.2
  192.0 1.2 collective-permute-done.2
  193.8 2.6 collective-permute-start.3
  196.5 12.6 %collective-permute-done.3 = bf16[2,132,1024]{2,0,1:T(2,128)(2,1)S(1)} collective-permute-done((bf16[2,132,1024]{2,0,1:T(2,128)(2,1)S(1)}, bf16[2,132,1024]{2,0,1:T(2,128)(2,1)S(1)}, u32[]{:S(2)}, u32[]{:S(2)}) %collective-permute-start.3) | collective-permute-done | bytes 540704 | tf_op jit(solution)/shard_map/ppermute | solution.py:27
  209.3 1.1 pad_maximum_fusion.1
  210.4 1.3 reshape.194
  211.7 9.7 %fusion.65 = bf16[528,1024]{1,0:T(8,128)(2,1)} fusion(bf16[2,1024,1024]{2,1,0:T(8,128)(2,1)} %param.28, f32[1024]{0:T(1024)} %bitcast.160, bf16[528,1024]{1,0:T(8,128)(2,1)S(1)} %reshape.194, bf16[2,1024,1024]{2,1,0:T(8,128)(2,1)} %param.26), kind=kOutput, calls=%fused_computation.85 | convolution fusion | flops 2250817536 | bytes 6361088 | tf_op jit(solution)/shard_map/dot_general | solution.py:282
  221.4 16.0 %fusion.3 = bf16[136,1024]{1,0:T(8,128)(2,1)S(1)} fusion(bf16[528,1024]{1,0:T(8,128)(2,1)} %fusion.65), kind=kCustom, calls=%all-reduce-scatter.3 | all-reduce-scatter fusion | flops 557057 | bytes 1360384
  237.5 1.3 collective-permute-start.7
  238.8 0.8 collective-permute-done.7
  239.9 0.9 add_convert_fusion
  240.9 10.9 %all_to_all.20 = bf16[4,132,256]{2,1,0:T(8,128)(2,1)S(1)} all-to-all(bf16[4,132,256]{2,1,0:T(8,128)(2,1)S(1)} %pad_maximum_fusion.4), channel_id=1, replica_groups=mesh['tm'=8,'tensor'=4] {'tensor'}, dimensions={0} | all-to-all | bytes 540672 | tf_op jit(solution)/shard_map/all_to_all | solution.py:293
  251.9 15.8 %all_to_all.21 = bf16[8,1,66,256]{3,2,1,0:T(8,128)(2,1)S(1)} all-to-all(bf16[8,1,66,256]{3,2,1,0:T(8,128)(2,1)S(1)} %bitcast.132), channel_id=1, replica_groups=mesh['tm'=8,'tensor'=4] {'tm'}, dimensions={0} | all-to-all | bytes 540672 | tf_op jit(solution)/shard_map/all_to_all | solution.py:295
  267.8 8.5 %all_to_all.22 = bf16[4,132,256]{2,1,0:T(8,128)(2,1)S(1)} all-to-all(bf16[4,132,256]{2,1,0:T(8,128)(2,1)S(1)} %reshape.195), channel_id=1, replica_groups=mesh['tm'=8,'tensor'=4] {'tensor'}, dimensions={0} | all-to-all | bytes 540672 | tf_op jit(solution)/shard_map/all_to_all | solution.py:297
  276.4 0.9 broadcast_in_dim_reshape.2
  (102 shorter events, 11.0 us)
Async XLA Ops:
  6.5 1.2 copy-start
  6.5 20.2 %copy-start.18 = (f32[2,3,256]{2,0,1:T(2,128)S(1)}, f32[2,3,256]{2,0,1:T(2,128)}, u32[]{:S(2)}) copy-start(f32[2,3,256]{2,0,1:T(2,128)} %param.21) | copy-start | bytes 18436
  6.5 20.8 %copy-start.12 = (f32[2,1024]{1,0:T(2,128)S(1)}, f32[2,1024]{1,0:T(2,128)}, u32[]{:S(2)}) copy-start(f32[2,1024]{1,0:T(2,128)} %param.25) | copy-start | bytes 24580
  6.5 21.4 %copy-start.13 = (f32[2,1024]{1,0:T(2,128)S(1)}, f32[2,1024]{1,0:T(2,128)}, u32[]{:S(2)}) copy-start(f32[2,1024]{1,0:T(2,128)} %param.24) | copy-start | bytes 24580
  6.5 22.0 %copy-start.14 = (f32[2,1024]{1,0:T(2,128)S(1)}, f32[2,1024]{1,0:T(2,128)}, u32[]{:S(2)}) copy-start(f32[2,1024]{1,0:T(2,128)} %param.19) | copy-start | bytes 24580
  6.5 22.6 %copy-start.15 = (f32[2,1024]{1,0:T(2,128)S(1)}, f32[2,1024]{1,0:T(2,128)}, u32[]{:S(2)}) copy-start(f32[2,1024]{1,0:T(2,128)} %param.18) | copy-start | bytes 24580
  8.6 16.9 %all-to-all-start = ((bf16[8,1,66,256]{3,2,1,0:T(8,128)(2,1)}), bf16[8,1,66,256]{3,2,1,0:T(8,128)(2,1)S(1)}, u32[]{:S(2)}, u32[]{:S(2)}) async-start(bf16[8,1,66,256]{3,2,1,0:T(8,128)(2,1)} %bitcast), calls=%async_computation | async-start | bytes 589824 | tf_op jit(solution)/shard_map/all_to_all | solution.py:221
  15.9 26.6 %all-gather.4.cloned.1.call-start = ((), (), s32[]{:S(2)}) async-start(), calls=%async_computation.4 | async-start | bytes 1351680 | tf_op jit(solution)/shard_map/all_gather | solution.py:223
  26.3 128.0 %all-gather.6.cloned.1.call-start = ((), (), s32[]{:S(2)}) async-start(), calls=%async_computation.5 | async-start | bytes 1392640 | tf_op jit(solution)/shard_map/all_gather | solution.py:291
  42.5 3.3 %copy-start.1 = (bf16[528,1024]{1,0:T(8,128)(2,1)S(1)}, bf16[528,1024]{1,0:T(8,128)(2,1)}, u32[]{:S(2)}) copy-start(bf16[528,1024]{1,0:T(8,128)(2,1)} %all-gather.4.cloned.1.call-done) | copy-start | bytes 3244036
  52.7 5.4 %copy-start.5 = (bf16[528,256]{0,1:T(8,128)(2,1)S(1)}, bf16[528,256]{0,1:T(8,128)(2,1)}, u32[]{:S(2)}) copy-start(bf16[528,256]{0,1:T(8,128)(2,1)} %copy.62) | copy-start | bytes 811012
  58.2 2.5 copy-start.2
  60.7 17.4 %copy-start.16 = (f32[2,1024]{1,0:T(2,128)S(1)}, f32[2,1024]{1,0:T(2,128)}, u32[]{:S(2)}) copy-start(f32[2,1024]{1,0:T(2,128)} %param.23) | copy-start | bytes 24580
  60.7 18.0 %copy-start.22 = (u32[32]{0:T(128)S(1)}, u32[32]{0:T(128)}, u32[]{:S(2)}) copy-start(u32[32]{0:T(128)} %constant.131) | copy-start | bytes 388
  76.6 3.3 %collective-permute-start.4 = (bf16[12,1024]{1,0:T(8,128)(2,1)S(1)}, bf16[12,1024]{1,0:T(8,128)(2,1)S(1)}, u32[]{:S(2)}, u32[]{:S(2)}) collective-permute-start(bf16[12,1024]{1,0:T(8,128)(2,1)S(1)} %slice.128), channel_id=1, source_target_pairs={{0,1},{1,2},{2,3},{4,5},{5,6},{6,7},{8,9},{9,10},{10,11},{12,13},{... | collective-permute-start | bytes 73736
  78.7 3.7 %copy-start.7 = (f32[1,1024]{1,0:T(1,128)}, f32[1,1024]{1,0:T(1,128)S(1)}, u32[]{:S(2)}) copy-start(f32[1,1024]{1,0:T(1,128)S(1)} %get-tuple-element.23) | copy-start | bytes 12292
  80.9 6.7 %copy-start.17 = (f32[2,1024]{1,0:T(2,128)S(1)}, f32[2,1024]{1,0:T(2,128)}, u32[]{:S(2)}) copy-start(f32[2,1024]{1,0:T(2,128)} %param.27) | copy-start | bytes 24580
  81.3 2.4 collective-permute-start
  86.0 14.9 %collective-permute-start.1 = (bf16[2,132,1024]{2,0,1:T(2,128)(2,1)}, bf16[2,132,1024]{2,0,1:T(2,128)(2,1)}, u32[]{:S(2)}, u32[]{:S(2)}) collective-permute-start(bf16[2,132,1024]{2,0,1:T(2,128)(2,1)} %copy.64), channel_id=1, source_target_pairs={{0,2},{1,3},{2,0},{3,1},{4,6},{5,7},{6,4},{7,5},{8,10},{9,11},{10,... | collective-permute-start | bytes 1622024 | tf_op jit(solution)/shard_map/ppermute | solution.py:27
  129.9 2.9 %collective-permute-start.5 = (bf16[12,1024]{1,0:T(8,128)(2,1)S(1)}, bf16[12,1024]{1,0:T(8,128)(2,1)S(1)}, u32[]{:S(2)}, u32[]{:S(2)}) collective-permute-start(bf16[12,1024]{1,0:T(8,128)(2,1)S(1)} %slice.129), channel_id=1, source_target_pairs={{0,1},{1,2},{2,3},{4,5},{5,6},{6,7},{8,9},{9,10},{10,11},{12,13},{... | collective-permute-start | bytes 73736
  134.8 21.6 %copy-start.10 = (f32[1,1024]{1,0:T(1,128)S(1)}, f32[1,1024]{1,0:T(1,128)}, u32[]{:S(2)}) copy-start(f32[1,1024]{1,0:T(1,128)} %get-tuple-element.21) | copy-start | bytes 12292
  134.8 21.6 %copy-start.11 = (f32[1,1024]{1,0:T(1,128)S(1)}, f32[1,1024]{1,0:T(1,128)}, u32[]{:S(2)}) copy-start(f32[1,1024]{1,0:T(1,128)} %get-tuple-element.19) | copy-start | bytes 12292
  155.7 1.2 copy-start.21
  156.4 2.9 %copy-start.20 = (f32[1,1,256]{2,0,1:T(1,128)S(1)}, f32[1,1,256]{2,0,1:T(1,128)}, u32[]{:S(2)}) copy-start(f32[1,1,256]{2,0,1:T(1,128)} %get-tuple-element.32) | copy-start | bytes 3076
  158.4 3.3 %copy-start.19 = (f32[1,1,256]{2,0,1:T(1,128)S(1)}, f32[1,1,256]{2,0,1:T(1,128)}, u32[]{:S(2)}) copy-start(f32[1,1,256]{2,0,1:T(1,128)} %get-tuple-element.31) | copy-start | bytes 3076
  163.5 5.4 %copy-start.4 = (bf16[528,256]{0,1:T(8,128)(2,1)S(1)}, bf16[528,256]{0,1:T(8,128)(2,1)}, u32[]{:S(2)}) copy-start(bf16[528,256]{0,1:T(8,128)(2,1)} %copy.69) | copy-start | bytes 811012
  168.9 2.5 copy-start.3
  171.4 18.4 %copy-start.6 = (f32[1,1024]{1,0:T(1,128)S(1)}, f32[1,1024]{1,0:T(1,128)}, u32[]{:S(2)}) copy-start(f32[1,1024]{1,0:T(1,128)} %get-tuple-element.24) | copy-start | bytes 12292
  171.4 18.9 %copy-start.8 = (f32[1,1024]{1,0:T(1,128)S(1)}, f32[1,1024]{1,0:T(1,128)}, u32[]{:S(2)}) copy-start(f32[1,1024]{1,0:T(1,128)} %get-tuple-element.28) | copy-start | bytes 12292
  171.4 18.9 %copy-start.9 = (f32[1,1024]{1,0:T(1,128)S(1)}, f32[1,1024]{1,0:T(1,128)}, u32[]{:S(2)}) copy-start(f32[1,1024]{1,0:T(1,128)} %get-tuple-element.26) | copy-start | bytes 12292
  187.3 2.1 collective-permute-start.6
  190.8 2.4 collective-permute-start.2
  193.8 15.2 %collective-permute-start.3 = (bf16[2,132,1024]{2,0,1:T(2,128)(2,1)S(1)}, bf16[2,132,1024]{2,0,1:T(2,128)(2,1)S(1)}, u32[]{:S(2)}, u32[]{:S(2)}) collective-permute-start(bf16[2,132,1024]{2,0,1:T(2,128)(2,1)S(1)} %copy.71), channel_id=1, source_target_pairs={{0,2},{1,3},{2,0},{3,1},{4,6},{5,7},{6,4},{7,5},{8,10},{9,11},{10,... | collective-permute-start | bytes 1622024 | tf_op jit(solution)/shard_map/ppermute | solution.py:27
  237.5 2.1 collective-permute-start.7
Sparse Core Ops, SparseCore 0:
  26.4 16.0 all-gather.3
  135.0 19.3 all-gather.5
